TPU v7x, 32 devices: a whole 2x2x4 slice. The times are simulated.
32 devices in a mesh: z: 4 (over z), y: 2 (over y), x: 4 (over x, core).
Axes of the slice: x: 2, y: 2, z: 4, core: 2. Of those that a mesh axis runs over, the one named last changes fastest.
Arguments:
- x_in: bfloat16 [65536, 4096], P(('z', 'y', 'x'))
- g_out: bfloat16 [65536, 512], P(('z', 'y', 'x'))
- w_in: bfloat16 [4096, 512], replicated
- w_up1: bfloat16 [512, 2048], replicated
- w_down1: bfloat16 [2048, 512], replicated
- w_up2: bfloat16 [512, 2048], replicated
- w_down2: bfloat16 [2048, 512], replicated
Outputs:
- output 1: bfloat16 [65536, 4096], P(('z', 'y', 'x'))
- output 2: float32 [4096, 512], replicated
- output 3: float32 [512, 2048], replicated
- output 4: float32 [2048, 512], replicated
- output 5: float32 [512, 2048], replicated
- output 6: float32 [2048, 512], replicated
All inputs are finite; a program needn't handle non-finite values.
Results may differ from a plain program's by a relative error of at most 0.0133355.
Values are sent between devices in bfloat16 or wider.
A program may use at most 1 GiB of HBM per device.

v0:
```python
import functools
import jax
import jax.numpy as jnp
from jax import lax
from jax.experimental import pallas as pl
from jax.experimental.pallas import tpu as pltpu
from jax.sharding import PartitionSpec as P

SQRT_HALF = 0.7071067811865476
INV_SQRT_TAU = 0.3989422804014327
MESH = pl.DeviceIdType.MESH
F32 = jnp.float32
BF16 = jnp.bfloat16

SIDE = 512
SLOTS = 8
STAGES = 10
LAG = (0, 1, 2, 3, 4, 5, 6, 7, 8, 9)


def gelu_value(pre_act):
    pre_wide = pre_act.astype(jnp.float32)
    return 0.5 * pre_wide * (1.0 + lax.erf(pre_wide * SQRT_HALF))


def gelu_slope(pre_act):
    pre_wide = pre_act.astype(jnp.float32)
    return 0.5 * (1.0 + lax.erf(pre_wide * SQRT_HALF)) + pre_wide * jnp.exp(-0.5 * pre_wide * pre_wide) * INV_SQRT_TAU


def plain_product(first_op, second_op):
    return lax.dot_general(first_op, second_op, (((1,), (0,)), ((), ())), preferred_element_type=jnp.float32)


def rows_contract(first_op, second_op):
    return lax.dot_general(first_op, second_op, (((0,), (0,)), ((), ())), preferred_element_type=jnp.float32)


def times_transposed(first_op, second_op):
    return lax.dot_general(first_op, second_op, (((1,), (1,)), ((), ())), preferred_element_type=jnp.float32)


def blocks_of(shape):
    rows, cols = shape
    return [(r, c) for r in range(0, rows, SIDE) for c in range(0, cols, SIDE)]


def add_rows(dst, dst_row, src, src_row, count, scale=None):
    step = 16

    def body(i, _):
        at = pl.ds(pl.multiple_of(dst_row + i * step, step), step)
        value = dst[at, :] + src[pl.ds(pl.multiple_of(src_row + i * step, step), step), :]
        dst[at, :] = value if scale is None else value * scale
        return 0

    lax.fori_loop(0, count // step, body, 0, unroll=True)


class Exchange:
    def __init__(self, total, scale, part, r0, r1, r2, r3, r4, send, recv, free, ready, emit):
        self.free = free
        self.total, self.scale, self.part = total, scale, part
        self.r0, self.r1, self.r2, self.r3, self.r4 = r0, r1, r2, r3, r4
        self.send, self.recv, self.ready, self.emit = send, recv, ready, emit
        z, y, x = lax.axis_index("z"), lax.axis_index("y"), lax.axis_index("x")
        core, chip = lax.rem(x, 2), x // 2
        self.z = z
        self.core_peer = (z, y, chip * 2 + 1 - core)
        self.x_peer = (z, y, (1 - chip) * 2 + core)
        self.y_peer = (z, 1 - y, x)
        self.inner = (z >= 1) & (z <= 2)
        self.outer = (z == 0) | (z == 3)
        self.mid = jnp.where(z >= 2, 1, 0)
        self.z_inner = (jnp.where(z == 0, 1, 2), y, x)
        self.z_peer = (jnp.where(z == 1, 2, 1), y, x)
        self.z_outer = (jnp.where(z == 1, 0, 3), y, x)
        half = SIDE // 2
        self.own = core * half
        self.other = (1 - core) * half
        self.a = self.own + chip * (half // 4)
        self.a_far = self.own + (1 - chip) * (half // 4)
        self.b = self.own + half // 2 + y * (half // 4)
        self.b_far = self.own + half // 2 + (1 - y) * (half // 4)

    def barrier(self):
        sem = pltpu.get_barrier_semaphore()
        for peer in (self.core_peer, self.x_peer, self.y_peer):
            pl.semaphore_signal(sem, inc=1, device_id=peer, device_id_type=MESH)

        @pl.when(self.inner)
        def _():
            pl.semaphore_signal(sem, inc=1, device_id=self.z_peer, device_id_type=MESH)
            pl.semaphore_signal(sem, inc=1, device_id=self.z_outer, device_id_type=MESH)
            pl.semaphore_wait(sem, 5)

        @pl.when(self.outer)
        def _():
            pl.semaphore_signal(sem, inc=1, device_id=self.z_inner, device_id_type=MESH)
            pl.semaphore_wait(sem, 4)

    def copy(self, kind, k, src, dst, peer):
        return pltpu.make_async_remote_copy(
            src_ref=src, dst_ref=dst, send_sem=self.send.at[kind, k], recv_sem=self.recv.at[kind, k],
            device_id=peer, device_id_type=MESH)

    def rows(self, k, start, count, align):
        return self.part.at[k, pl.ds(pl.multiple_of(start, align), count), :]

    def c_core(self, k):
        return self.copy(0, k, self.rows(k, self.other, 256, 256), self.r0.at[lax.rem(k, SLOTS)], self.core_peer)

    def c_side(self, k):
        slot = lax.rem(k, SLOTS)
        return (self.copy(1, k, self.rows(k, self.a_far, 64, 64), self.r1.at[slot, pl.ds(0, 64), :], self.x_peer),
                self.copy(2, k, self.rows(k, self.b_far, 64, 64), self.r1.at[slot, pl.ds(64, 64), :], self.y_peer))

    def c_in(self, k):
        slot = lax.rem(k, SLOTS)
        return (self.copy(3, k, self.rows(k, self.a, 64, 64), self.r2.at[slot, pl.ds(0, 64), :], self.z_inner),
                self.copy(4, k, self.rows(k, self.b, 64, 64), self.r2.at[slot, pl.ds(64, 64), :], self.z_inner))

    def c_pair(self, k):
        slot, far = lax.rem(k, SLOTS), (1 - self.mid) * 32
        return (self.copy(5, k, self.rows(k, self.a + far, 32, 32), self.r3.at[slot, pl.ds(0, 32), :], self.z_peer),
                self.copy(6, k, self.rows(k, self.b + far, 32, 32), self.r3.at[slot, pl.ds(32, 32), :], self.z_peer))

    def c_turn(self, k):
        slot, near = lax.rem(k, SLOTS), self.mid * 32
        return (self.copy(7, k, self.rows(k, self.a + near, 32, 32), self.r4.at[slot, pl.ds(0, 32), :], self.y_peer),
                self.copy(8, k, self.rows(k, self.b + near, 32, 32), self.r4.at[slot, pl.ds(32, 32), :], self.x_peer))

    def c_back(self, k):
        near = self.mid * 32
        a, b = self.rows(k, self.a + near, 32, 32), self.rows(k, self.b + near, 32, 32)
        return (self.copy(9, k, a, a, self.z_peer), self.copy(10, k, b, b, self.z_peer))

    def c_out(self, k, kind, at):
        a, b = self.rows(k, self.a + at, 32, 32), self.rows(k, self.b + at, 32, 32)
        return (self.copy(kind, k, a, a, self.z_outer), self.copy(kind + 1, k, b, b, self.z_outer))

    def c_wide(self, k):
        a, b = self.rows(k, self.a, 64, 64), self.rows(k, self.b, 64, 64)
        return (self.copy(15, k, a, a, self.x_peer), self.copy(16, k, b, b, self.y_peer))

    def c_full(self, k):
        half = self.rows(k, self.own, 256, 256)
        return self.copy(17, k, half, half, self.core_peer)

    def release(self, kind, peer):
        pl.semaphore_signal(self.free.at[kind], inc=1, device_id=peer, device_id_type=MESH)

    def stage(self, s, k):
        part, slot = self.part.at[k], lax.rem(k, SLOTS)
        if s == 0:
            self.ready(k)
            self.c_core(k).start()
        elif s == 1:
            self.c_core(k).wait()
            self.release(0, self.core_peer)
            r0 = self.r0.at[slot]
            add_rows(part, self.own, r0, 0, 256)
            for c in self.c_side(k):
                c.start()
        elif s == 2:
            for c in self.c_side(k):
                c.wait()
            add_rows(part, self.a, self.r1.at[slot], 0, 64)
            add_rows(part, self.b, self.r1.at[slot], 64, 64)

            @pl.when(self.outer)
            def _():
                for c in self.c_in(k):
                    c.start()
        elif s == 3:
            @pl.when(self.inner)
            def _():
                for c in self.c_in(k):
                    c.wait_recv()
                add_rows(part, self.a, self.r2.at[slot], 0, 64)
                add_rows(part, self.b, self.r2.at[slot], 64, 64)
                for c in self.c_pair(k):
                    c.start()

            @pl.when(self.outer)
            def _():
                for c in self.c_in(k):
                    c.wait_send()
                self.release(1, self.z_inner)
        elif s == 4:
            @pl.when(self.inner)
            def _():
                for c in self.c_pair(k):
                    c.wait()
                self.release(2, self.z_peer)
                add_rows(part, self.a + self.mid * 32, self.r3.at[slot], 0, 32)
                add_rows(part, self.b + self.mid * 32, self.r3.at[slot], 32, 32)
                for c in self.c_turn(k):
                    c.start()
        elif s == 5:
            @pl.when(self.inner)
            def _():
                for c in self.c_turn(k):
                    c.wait()
                add_rows(part, self.a + self.mid * 32, self.r4.at[slot], 0, 32, self.scale)
                add_rows(part, self.b + self.mid * 32, self.r4.at[slot], 32, 32, self.scale)
                pl.semaphore_wait(self.free.at[1], 1)
                pl.semaphore_wait(self.free.at[2], 1)
                for c in self.c_back(k) + self.c_out(k, 11, self.mid * 32):
                    c.start()
        elif s == 6:
            @pl.when(self.inner)
            def _():
                for c in self.c_back(k):
                    c.wait_recv()
                for c in self.c_out(k, 13, (1 - self.mid) * 32) + self.c_wide(k):
                    c.start()
        elif s == 7:
            @pl.when(self.outer)
            def _():
                for c in self.c_out(k, 11, 0) + self.c_out(k, 13, 0):
                    c.wait_recv()
                for c in self.c_wide(k):
                    c.start()
        elif s == 8:
            for c in self.c_wide(k):
                c.wait_recv()
            pl.semaphore_wait(self.free.at[0], 1)
            self.c_full(k).start()
        elif s == 9:
            self.c_full(k).wait_recv()
            self.emit(k)

    def tick(self, t):
        for s in reversed(range(STAGES)):
            k = t - LAG[s]

            @pl.when((k >= 0) & (k < self.total))
            def _():
                self.stage(s, k)

    def drain(self):
        def body(k, _):
            for c in self.c_wide(k):
                c.wait_send()
            self.c_full(k).wait_send()

            @pl.when(self.inner)
            def _():
                for c in self.c_back(k) + self.c_out(k, 11, 0) + self.c_out(k, 13, 0):
                    c.wait_send()
            return 0

        lax.fori_loop(0, self.total, body, 0)


def backward_kernel(groups, scale, *refs):
    (dw4, g_in, a3, h2, a1, h1, m_in, x0, w4, w3, w2, w1), refs = refs[:12], refs[12:]
    outs, dm_out, refs = refs[:5], refs[5], refs[6:]
    part, r0, r1, r2, r3, r4, d_act, w_down, w_up, g_buf, lhs, dh2, col = refs[:13]
    send, recv, free, load_sem, store_sem, side_sem, col_sem = refs[13:]
    total = sum(len(blocks_of(g)) for g in groups)

    def load(n, src, dst):
        return pltpu.make_async_copy(src, dst, side_sem.at[n])

    streams = ((a3, 0, 4), (h1, 4, 4), (a1, 8, 4), (x0, 12, 8))

    def fetch(n):
        for ref, first, count in streams:
            @pl.when((n >= first) & (n < first + count))
            def _():
                at = pl.ds(pl.multiple_of((n - first) * SIDE, SIDE), SIDE)
                slot = lax.rem(n, 2)
                pltpu.make_async_copy(ref.at[:, at], col.at[slot], col_sem.at[slot]).start()

    def fetched(n):
        slot = lax.rem(n, 2)
        pltpu.make_async_copy(a3.at[:, pl.ds(0, SIDE)], col.at[slot], col_sem.at[slot]).wait()
        return col.at[slot]

    load(0, g_in, g_buf).start()
    load(1, w4, w_down).start()
    fetch(0)
    load(2, h2, lhs).start()
    fetch(1)
    load(3, w3, w_up).start()
    for k in range(4):
        pltpu.make_async_copy(dw4.at[pl.ds(k * SIDE, SIDE), :], part.at[k], load_sem.at[k]).start()

    def ready(k):
        @pl.when(k < 4)
        def _():
            pltpu.make_async_copy(dw4.at[pl.ds(0, SIDE), :], part.at[k], load_sem.at[k]).wait()

    def emit(k):
        first = 0
        for ref, shape in zip(outs, groups):
            count = len(blocks_of(shape))
            base = first

            @pl.when((k >= base) & (k < base + count))
            def _():
                at = pl.multiple_of((k - base) * SIDE, SIDE)
                dst = ref.at[pl.ds(at, SIDE), :] if shape[1] == SIDE else ref.at[:, pl.ds(at, SIDE)]
                pltpu.make_async_copy(part.at[k], dst, store_sem.at[k]).start()
            first += count

    def grad_block(k, left, right, right_cols):
        for piece in range(2):
            rows = pl.ds(piece * 1024, 1024)
            value = rows_contract(left[rows, :], right[rows, right_cols])
            if piece == 0:
                part[k] = value
            else:
                part[k] += value

    def slope_block(j, grad, act):
        at = pl.ds(pl.multiple_of(j * SIDE, SIDE), SIDE)

        def body(t, _):
            rows = pl.ds(pl.multiple_of(t * 256, 256), 256)
            d_out = times_transposed(grad[rows, :], w_down[at, :]).astype(BF16)
            d_act[rows, at] = (d_out.astype(F32) * gelu_slope(act[rows, :])).astype(BF16)
            return 0

        lax.fori_loop(0, 8, body, 0)
        return at

    def back_rows(add, dst):
        def body(t, _):
            rows = pl.ds(pl.multiple_of(t * 512, 512), 512)
            dst[rows, :] = (times_transposed(d_act[rows, :], w_up[...]) + add[rows, :].astype(F32)).astype(BF16)
            return 0

        lax.fori_loop(0, 4, body, 0)

    def compute(i):
        @pl.when(i == 1)
        def _():
            load(0, g_in, g_buf).wait()
            load(1, w4, w_down).wait()
            load(2, h2, lhs).wait()

        @pl.when(i == 8)
        def _():
            load(4, w2, w_down).wait()
            load(5, m_in, lhs).wait()

        for first, n0, grad, k0 in ((1, 0, g_buf, 4), (8, 8, dh2, 12)):
            @pl.when((i >= first) & (i < first + 4))
            def _():
                j = i - first
                act = fetched(n0 + j)
                at = slope_block(j, grad, act)
                fetch(n0 + j + 2)
                grad_block(k0 + j, lhs, d_act, at)

        @pl.when(i == 4)
        def _():
            load(4, w2, w_down).start()
            load(5, m_in, lhs).start()

        @pl.when(i == 5)
        def _():
            load(3, w3, w_up).wait()
            back_rows(g_buf, dh2)
            load(6, w1, w_up).start()

        @pl.when(i == 12)
        def _():
            load(6, w1, w_up).wait()
            back_rows(dh2, g_buf)
            load(7, g_buf, dm_out).start()

        for first, count, n0, right, k0 in ((6, 2, 4, dh2, 8), (13, 4, 12, g_buf, 16)):
            @pl.when((i >= first) & (i < first + count))
            def _():
                def body(e, _):
                    j = (i - first) * 2 + e
                    left = fetched(n0 + j)
                    grad_block(k0 + j, left, right, slice(None))
                    fetch(n0 + j + 2)
                    return 0

                lax.fori_loop(0, 2, body, 0)

    ex = Exchange(total, scale, part, r0, r1, r2, r3, r4, send, recv, free, ready, emit)
    ex.barrier()

    def step(i, _):
        compute(i)
        ex.tick(i)
        return 0

    lax.fori_loop(0, total + LAG[-1], step, 0)
    ex.drain()
    load(7, g_buf, dm_out).wait()

    def stored(k, _):
        pltpu.make_async_copy(part.at[k], outs[0].at[pl.ds(0, SIDE), pl.ds(0, SIDE)], store_sem.at[k]).wait()
        return 0

    lax.fori_loop(0, total, stored, 0)


def backward(dw4, g, a3, h2, a1, h1, m, x0, w4, w3, w2, w1, groups, scale):
    total = sum(len(blocks_of(g)) for g in groups)
    any_spec = pl.BlockSpec(memory_space=pl.ANY)
    rows, wide = a3.shape
    return pl.pallas_call(
        functools.partial(backward_kernel, groups, scale),
        out_shape=[jax.ShapeDtypeStruct(g, F32) for g in groups] + [jax.ShapeDtypeStruct((rows, SIDE), BF16)],
        in_specs=[any_spec] * 12,
        out_specs=[any_spec] * 6,
        scratch_shapes=[
            pltpu.VMEM((total, SIDE, SIDE), F32),
            pltpu.VMEM((SLOTS, 256, SIDE), F32),
            pltpu.VMEM((SLOTS, 128, SIDE), F32),
            pltpu.VMEM((SLOTS, 128, SIDE), F32),
            pltpu.VMEM((SLOTS, 64, SIDE), F32),
            pltpu.VMEM((SLOTS, 64, SIDE), F32),
            pltpu.VMEM((rows, wide), BF16),
            pltpu.VMEM((wide, SIDE), BF16),
            pltpu.VMEM((SIDE, wide), BF16),
            pltpu.VMEM((rows, SIDE), BF16),
            pltpu.VMEM((rows, SIDE), BF16),
            pltpu.VMEM((rows, SIDE), BF16),
            pltpu.VMEM((2, rows, SIDE), BF16),
            pltpu.SemaphoreType.DMA((18, total)),
            pltpu.SemaphoreType.DMA((18, total)),
            pltpu.SemaphoreType.REGULAR((3,)),
            pltpu.SemaphoreType.DMA((4,)),
            pltpu.SemaphoreType.DMA((total,)),
            pltpu.SemaphoreType.DMA((8,)),
            pltpu.SemaphoreType.DMA((2,)),
        ],
        compiler_params=pltpu.CompilerParams(
            collective_id=0, has_side_effects=True, vmem_limit_bytes=67 * 1000 * 1000),
        name="backward_and_mean",
    )(dw4, g, a3, h2, a1, h1, m, x0, w4, w3, w2, w1)


def finish_kernel(groups, dm, w0, *refs):
    ins, dx, outs = refs[:5], refs[5], refs[6:11]
    through, rows_out, in_sem, out_sem, dx_sem = refs[11:]
    moves = [(src, dst, r) for src, dst, shape in zip(ins, outs, groups) for r in range(0, shape[0], 128 if shape[1] > SIDE else SIDE)]
    depth = 6

    def views(n):
        src, dst, r = moves[n]
        count = 128 if src.shape[1] > SIDE else SIDE
        buf = through[0] if src.shape[1] == SIDE else through[1]
        return src.at[pl.ds(r, count), :], buf.at[n % depth], dst.at[pl.ds(r, count), :]

    def start_in(n):
        src, mid, _ = views(n)
        pltpu.make_async_copy(src, mid, in_sem.at[n]).start()

    def pass_on(n):
        src, mid, dst = views(n)
        pltpu.make_async_copy(src, mid, in_sem.at[n]).wait()
        pltpu.make_async_copy(mid, dst, out_sem.at[n]).start()

    def passed(n):
        _, mid, dst = views(n)
        pltpu.make_async_copy(mid, dst, out_sem.at[n]).wait()

    def dx_copy(i):
        return pltpu.make_async_copy(rows_out.at[i % 2], dx.at[pl.ds(i * 128, 128), :], dx_sem.at[i % 2])

    for n in range(depth // 2):
        start_in(n)
    steps, width = 16, 4096
    done = 0
    for i in range(steps):
        for n in range(done, (i + 1) * len(moves) // steps):
            if n + depth // 2 < len(moves):
                if n - depth // 2 >= 0:
                    passed(n - depth // 2)
                start_in(n + depth // 2)
            pass_on(n)
            done = n + 1
        if i >= 2:
            dx_copy(i - 2).wait()

        def column(j, _):
            at = pl.ds(pl.multiple_of(j * 1024, 1024), 1024)
            rows_out[i % 2, :, at] = times_transposed(dm[pl.ds(i * 128, 128), :], w0[at, :]).astype(BF16)
            return 0

        lax.fori_loop(0, width // 1024, column, 0)
        dx_copy(i).start()
    for i in (steps - 2, steps - 1):
        dx_copy(i).wait()
    for n in range(max(0, len(moves) - depth), len(moves)):
        passed(n)


def solution(mesh):
    batch_axes = ("z", "y", "x")
    scale = 1.0 / mesh.size
    row_spec = P(batch_axes, None)
    full_spec = P(None, None)

    def device_step(x_in, g_out, w_in, w_up1, w_down1, w_up2, w_down2):
        x_mid = plain_product(x_in, w_in).astype(jnp.bfloat16)
        pre_one = plain_product(x_mid, w_up1).astype(jnp.bfloat16)
        act_one = gelu_value(pre_one).astype(jnp.bfloat16)
        hid_two = (plain_product(act_one, w_down1) + x_mid.astype(jnp.float32)).astype(jnp.bfloat16)
        pre_three = plain_product(hid_two, w_up2).astype(jnp.bfloat16)
        act_three = gelu_value(pre_three).astype(jnp.bfloat16)
        dw_down2 = rows_contract(act_three, g_out)
        groups = (dw_down2.shape, w_up2.shape, w_down1.shape, w_up1.shape, w_in.shape)
        dw_down2, dw_up2, dw_down1, dw_up1, dw_in, d_mid = backward(
            dw_down2, g_out, pre_three, hid_two, pre_one, act_one, x_mid, x_in, w_down2, w_up2, w_down1, w_up1, groups, scale)
        dx_rows = times_transposed(d_mid, w_in).astype(jnp.bfloat16)
        return dx_rows, dw_in, dw_up1, dw_down1, dw_up2, dw_down2

    return jax.shard_map(
        device_step,
        mesh=mesh,
        in_specs=(row_spec, row_spec, full_spec, full_spec, full_spec, full_spec, full_spec),
        out_specs=(row_spec, full_spec, full_spec, full_spec, full_spec, full_spec),
        check_vma=False,
    )
```

profile of v0, /device:TPU:1, one launch (start us, length us, event | category | flops | bytes accessed | tf_op | source)
XLA Modules:
  0.0 297.8 jit_solution(11528879547732551972)
XLA Ops:
  0.6 0.0 copy-start.7
  0.6 13.7 %fusion.16.refs_6_ = bf16[2048,512]{1,0:T(8,128)(2,1)S(1)} fusion(bf16[2048,4096]{1,0:T(8,128)(2,1)} %refs_7_.1, bf16[4096,512]{1,0:T(8,128)(2,1)} %param.9), kind=kOutput, calls=%fused_computation.23 | convolution fusion | flops 8589934592 | bytes 23068672 | tf_op jit(solution)/shard_map/dot_general | solution.py:32
  14.4 0.0 copy-done.7
  14.4 0.0 copy-start.10
  14.4 0.0 copy-start.8
  14.4 7.5 %fusion.1 = (bf16[2048,2048]{1,0:T(8,128)(2,1)S(1)}, bf16[2048,2048]{1,0:T(8,128)(2,1)}) fusion(bf16[2048,512]{1,0:T(8,128)(2,1)S(1)} %fusion.16.refs_6_, bf16[512,2048]{1,0:T(8,128)(2,1)S(1)} %copy-done.7), kind=kOutput, calls=%fused_computation.5 | convolution fusion | flops 4324327424 | bytes 20971520 | tf_op jit(solution)/shard_map/dot_general | solution.py:32
  21.9 0.0 copy-start
  21.9 0.0 copy-done.10
  21.9 3.2 %copy-done = bf16[2048,2048]{1,0:T(8,128)(2,1)} copy-done((bf16[2048,2048]{1,0:T(8,128)(2,1)}, bf16[2048,2048]{1,0:T(8,128)(2,1)S(1)}, u32[]{:S(2)}) %copy-start) | copy-done | bytes 8388632
  25.1 0.0 copy-done.8
  25.1 0.0 copy-start.9
  25.2 4.7 %fusion.12.refs_3_ = bf16[2048,512]{1,0:T(8,128)(2,1)S(1)} fusion(bf16[2048,512]{1,0:T(8,128)(2,1)S(1)} %fusion.16.refs_6_, bf16[2048,2048]{1,0:T(8,128)(2,1)S(1)} %get-tuple-element.18.refs_5_, bf16[2048,512]{1,0:T(8,128)(2,1)S(1)} %copy-done.8), kind=kOutput, calls=%fused_computation.19 | convolution fusion | flops 4298113024 | bytes 14680064 | tf_op jit(solution)/shard_map/dot_general | solution.py:32
  29.8 0.0 copy-done.9
  29.8 0.0 copy-start.11
  29.8 0.0 copy-start.6
  29.9 4.8 %convolution_convert_fusion.1.refs_2_ = bf16[2048,2048]{1,0:T(8,128)(2,1)S(1)} fusion(bf16[2048,512]{1,0:T(8,128)(2,1)S(1)} %fusion.12.refs_3_, bf16[512,2048]{1,0:T(8,128)(2,1)S(1)} %copy-done.9), kind=kOutput, calls=%fused_computation.14 | convolution fusion | flops 4299161600 | bytes 12582912 | tf_op jit(solution)/shard_map/dot_general | solution.py:32
  34.7 0.0 copy-done.11
  34.7 0.0 copy-start.1
  34.7 3.4 %copy-done.1 = bf16[2048,2048]{1,0:T(8,128)(2,1)} copy-done((bf16[2048,2048]{1,0:T(8,128)(2,1)}, bf16[2048,2048]{1,0:T(8,128)(2,1)S(1)}, u32[]{:S(2)}) %copy-start.1) | copy-done | bytes 8388632
  38.1 0.0 copy-done.6
  38.1 6.3 %fusion.8.refs_0_ = f32[2048,512]{1,0:T(8,128)} fusion(bf16[2048,512]{1,0:T(8,128)(2,1)S(1)} %copy-done.6, bf16[2048,2048]{1,0:T(8,128)(2,1)S(1)} %convolution_convert_fusion.1.refs_2_), kind=kOutput, calls=%fused_computation.13 | convolution fusion | flops 4320133120 | bytes 14680064 | tf_op jit(solution)/shard_map/dot_general | solution.py:36
  44.4 217.2 %backward_and_mean.1 = (f32[2048,512]{1,0:T(8,128)}, f32[512,2048]{1,0:T(8,128)}, f32[2048,512]{1,0:T(8,128)}, f32[512,2048]{1,0:T(8,128)}, f32[4096,512]{1,0:T(8,128)}, /*index=5*/bf16[2048,512]{1,0:T(8,128)(2,1)}) custom-call(f32[2048,512]{1,0:T(8,128)} %fusion.8.refs_0_, bf16[2048,512]{1,0:T(8,128)(2,1)} %refs_1_.1, bf16[2048,2048]{1,0:T(8,128)(2,1)} %copy-done.1, ...), custom_call_target="tpu_custom_call" | custom-call | tf_op jit(solution)/shard_map/backward_and_mean/pallas_call | solution.py:411
  261.7 15.0 %convolution_convert_fusion = bf16[2048,4096]{1,0:T(8,128)(2,1)} fusion(bf16[2048,512]{1,0:T(8,128)(2,1)} %get-tuple-element.12, bf16[4096,512]{1,0:T(8,128)(2,1)} %param.9), kind=kOutput, calls=%fused_computation.12 | convolution fusion | flops 8598323200 | bytes 23068672 | tf_op jit(solution)/shard_map/dot_general | solution.py:40
  276.7 0.0 copy-start.5
  276.7 7.9 %copy.18 = f32[4096,512]{1,0:T(8,128)} copy(f32[4096,512]{1,0:T(8,128)} %get-tuple-element.27) | data formatting | bytes 16777216
  284.6 0.0 copy-done.5
  284.7 0.0 copy-start.4
  284.7 2.1 copy.19
  286.8 1.6 copy-done.4
  288.4 0.0 copy-start.3
  288.4 2.1 copy.20
  290.5 1.6 copy-done.3
  292.1 0.0 copy-start.2
  292.1 2.1 copy.21
  294.2 1.6 copy-done.2
  295.8 2.0 copy.22
Async XLA Ops:
  0.6 13.7 %copy-start.7 = (bf16[512,2048]{1,0:T(8,128)(2,1)S(1)}, bf16[512,2048]{1,0:T(8,128)(2,1)}, u32[]{:S(2)}) copy-start(bf16[512,2048]{1,0:T(8,128)(2,1)} %refs_11_.1) | copy-start | bytes 6291460
  14.4 7.6 %copy-start.10 = (bf16[2048,512]{1,0:T(8,128)(2,1)}, bf16[2048,512]{1,0:T(8,128)(2,1)S(1)}, u32[]{:S(2)}) copy-start(bf16[2048,512]{1,0:T(8,128)(2,1)S(1)} %fusion.16.refs_6_) | copy-start | bytes 6291460
  14.4 10.8 %copy-start.8 = (bf16[2048,512]{1,0:T(8,128)(2,1)S(1)}, bf16[2048,512]{1,0:T(8,128)(2,1)}, u32[]{:S(2)}) copy-start(bf16[2048,512]{1,0:T(8,128)(2,1)} %refs_10_.1) | copy-start | bytes 6291460
  21.9 3.2 %copy-start = (bf16[2048,2048]{1,0:T(8,128)(2,1)}, bf16[2048,2048]{1,0:T(8,128)(2,1)S(1)}, u32[]{:S(2)}) copy-start(bf16[2048,2048]{1,0:T(8,128)(2,1)S(1)} %get-tuple-element.18.refs_5_) | copy-start | bytes 25165828
  25.1 4.7 %copy-start.9 = (bf16[512,2048]{1,0:T(8,128)(2,1)S(1)}, bf16[512,2048]{1,0:T(8,128)(2,1)}, u32[]{:S(2)}) copy-start(bf16[512,2048]{1,0:T(8,128)(2,1)} %refs_9_.1) | copy-start | bytes 6291460
  29.8 4.9 %copy-start.11 = (bf16[2048,512]{1,0:T(8,128)(2,1)}, bf16[2048,512]{1,0:T(8,128)(2,1)S(1)}, u32[]{:S(2)}) copy-start(bf16[2048,512]{1,0:T(8,128)(2,1)S(1)} %fusion.12.refs_3_) | copy-start | bytes 6291460
  29.8 8.3 %copy-start.6 = (bf16[2048,512]{1,0:T(8,128)(2,1)S(1)}, bf16[2048,512]{1,0:T(8,128)(2,1)}, u32[]{:S(2)}) copy-start(bf16[2048,512]{1,0:T(8,128)(2,1)} %refs_1_.1) | copy-start | bytes 6291460
  34.7 3.4 %copy-start.1 = (bf16[2048,2048]{1,0:T(8,128)(2,1)}, bf16[2048,2048]{1,0:T(8,128)(2,1)S(1)}, u32[]{:S(2)}) copy-start(bf16[2048,2048]{1,0:T(8,128)(2,1)S(1)} %convolution_convert_fusion.1.refs_2_) | copy-start | bytes 25165828
  276.7 7.9 %copy-start.5 = (f32[512,2048]{1,0:T(8,128)S(1)}, f32[512,2048]{1,0:T(8,128)}, u32[]{:S(2)}) copy-start(f32[512,2048]{1,0:T(8,128)} %get-tuple-element.28) | copy-start | bytes 12582916
  284.7 3.7 %copy-start.4 = (f32[2048,512]{1,0:T(8,128)S(1)}, f32[2048,512]{1,0:T(8,128)}, u32[]{:S(2)}) copy-start(f32[2048,512]{1,0:T(8,128)} %get-tuple-element.29) | copy-start | bytes 12582916
  288.4 3.7 %copy-start.3 = (f32[512,2048]{1,0:T(8,128)S(1)}, f32[512,2048]{1,0:T(8,128)}, u32[]{:S(2)}) copy-start(f32[512,2048]{1,0:T(8,128)} %get-tuple-element.30) | copy-start | bytes 12582916
  292.1 3.7 %copy-start.2 = (f32[2048,512]{1,0:T(8,128)S(1)}, f32[2048,512]{1,0:T(8,128)}, u32[]{:S(2)}) copy-start(f32[2048,512]{1,0:T(8,128)} %get-tuple-element.31) | copy-start | bytes 12582916
where the time goes:
time: 298 us
  Pallas kernels  217 us (73%)
  matrix products  52.1 us (17%)
  local copies, waits for them, and re-layouts  27.7 us (9%)
    pallas_call x1, Pallas kernels, backward(): pl.pallas_call(functools.partial(backward_kernel, groups, scale), out_sha...  217 us
    dot_general x4, matrix products, plain_product(): lax.dot_general(first_op, second_op, (((1,), (0,)), ((), ())), preferred_...  30.7 us
    unnamed x29, local copies, waits for them, and re-layouts  27.7 us
    dot_general x1, matrix products, times_transposed(): lax.dot_general(first_op, second_op, (((1,), (1,)), ((), ())), preferred_...  15 us
    dot_general x1, matrix products, rows_contract(): lax.dot_general(first_op, second_op, (((0,), (0,)), ((), ())), preferred_...  6.34 us

commit v1 on v0

v1 whole, which is shorter than its diff:
```python
import functools
import jax
import jax.numpy as jnp
from jax import lax
from jax.experimental import pallas as pl
from jax.experimental.pallas import tpu as pltpu
from jax.sharding import PartitionSpec as P

SQRT_HALF = 0.7071067811865476
INV_SQRT_TAU = 0.3989422804014327
MESH = pl.DeviceIdType.MESH
F32 = jnp.float32
BF16 = jnp.bfloat16

SIDE = 512
UNIT = SIDE // 2
SLOTS = 8
TURNS = 16
LAG = (0, 2, 4, 6, 8, 10, 12, 14, 16, 18, 20, 22)


def gelu_value(pre_act):
    pre_wide = pre_act.astype(jnp.float32)
    return 0.5 * pre_wide * (1.0 + lax.erf(pre_wide * SQRT_HALF))


def gelu_slope(pre_act):
    pre_wide = pre_act.astype(jnp.float32)
    return 0.5 * (1.0 + lax.erf(pre_wide * SQRT_HALF)) + pre_wide * jnp.exp(-0.5 * pre_wide * pre_wide) * INV_SQRT_TAU


def plain_product(first_op, second_op):
    return lax.dot_general(first_op, second_op, (((1,), (0,)), ((), ())), preferred_element_type=jnp.float32)


def rows_contract(first_op, second_op):
    return lax.dot_general(first_op, second_op, (((0,), (0,)), ((), ())), preferred_element_type=jnp.float32)


def times_transposed(first_op, second_op):
    return lax.dot_general(first_op, second_op, (((1,), (1,)), ((), ())), preferred_element_type=jnp.float32)


def blocks_of(shape):
    rows, cols = shape
    return [(r, c) for r in range(0, rows, SIDE) for c in range(0, cols, SIDE)]


class Exchange:
    def __init__(self, total, scale, part, r0, r1, r2, r3, r4, send, recv, free, ready, emit):
        self.total, self.scale, self.part = total, scale, part
        self.r0, self.r1, self.r2, self.r3, self.r4 = r0, r1, r2, r3, r4
        self.send, self.recv, self.free, self.ready, self.emit = send, recv, free, ready, emit
        z, y, x = lax.axis_index("z"), lax.axis_index("y"), lax.axis_index("x")
        core, chip = lax.rem(x, 2), x // 2
        self.core_peer = (z, y, chip * 2 + 1 - core)
        self.x_peer = (z, y, (1 - chip) * 2 + core)
        self.y_peer = (z, 1 - y, x)
        self.inner = (z >= 1) & (z <= 2)
        self.outer = (z == 0) | (z == 3)
        self.z_inner = (jnp.where(z == 0, 1, 2), y, x)
        self.z_peer = (jnp.where(z == 1, 2, 1), y, x)
        self.z_outer = (jnp.where(z == 1, 0, 3), y, x)
        half, self.q = UNIT // 2, UNIT // 8
        n = self.n = self.q // 4
        self.half = half
        self.own = core * half
        self.other = (1 - core) * half
        self.a = self.own + chip * self.q
        self.a_far = self.own + (1 - chip) * self.q
        self.b = self.own + half // 2 + y * self.q
        self.b_far = self.own + half // 2 + (1 - y) * self.q
        high = jnp.where(z >= 2, 1, 0)
        self.to_in = n * (1 - high)
        self.to_pair = 2 * n * (1 - high)
        self.from_pair = 2 * n * high
        self.to_out = 3 * n * high
        self.mine = n * z
        self.twin = n * (3 - z)
        self.far = 3 * n * (1 - high)

    def barrier(self):
        sem = pltpu.get_barrier_semaphore()
        for peer in (self.core_peer, self.x_peer, self.y_peer):
            pl.semaphore_signal(sem, inc=1, device_id=peer, device_id_type=MESH)

        @pl.when(self.inner)
        def _():
            pl.semaphore_signal(sem, inc=1, device_id=self.z_peer, device_id_type=MESH)
            pl.semaphore_signal(sem, inc=1, device_id=self.z_outer, device_id_type=MESH)
            pl.semaphore_wait(sem, 5)

        @pl.when(self.outer)
        def _():
            pl.semaphore_signal(sem, inc=1, device_id=self.z_inner, device_id_type=MESH)
            pl.semaphore_wait(sem, 4)

    def copy(self, kind, k, src, dst, peer):
        turn = lax.rem(k, TURNS)
        return pltpu.make_async_remote_copy(
            src_ref=src, dst_ref=dst, send_sem=self.send.at[kind, turn], recv_sem=self.recv.at[kind, turn],
            device_id=peer, device_id_type=MESH)

    def rows(self, k, start, count):
        at = pl.multiple_of(lax.rem(k, 2) * UNIT + start, 8)
        return self.part.at[k // 2, pl.ds(at, count), :]

    def both(self, kind, k, at, count, peer, into=None):
        slot, out = lax.rem(k, SLOTS), []
        for e, base in enumerate((self.a, self.b)):
            src = self.rows(k, base + at, count)
            dst = src if into is None else into.at[slot, pl.ds(pl.multiple_of(e * self.q + at, 8), count), :]
            out.append(self.copy(kind + e, k, src, dst, peer))
        return out

    def c_core(self, k):
        return [self.copy(0, k, self.rows(k, self.other, self.half), self.r0.at[lax.rem(k, SLOTS)], self.core_peer)]

    def c_side(self, k):
        slot = lax.rem(k, SLOTS)
        return [self.copy(1, k, self.rows(k, self.a_far, self.q), self.r1.at[slot, pl.ds(0, self.q), :], self.x_peer),
                self.copy(2, k, self.rows(k, self.b_far, self.q), self.r1.at[slot, pl.ds(self.q, self.q), :], self.y_peer)]

    def c_in(self, k):
        return self.both(3, k, self.to_in, 3 * self.n, self.z_inner, self.r2)

    def c_pair(self, k):
        return self.both(5, k, self.to_pair, 2 * self.n, self.z_peer, self.r3)

    def c_end(self, k):
        return self.both(7, k, self.to_out, self.n, self.z_outer, self.r2)

    def c_turn(self, k):
        slot, n = lax.rem(k, SLOTS), self.n
        return [self.copy(9, k, self.rows(k, self.a + self.mine, n), self.r4.at[slot, pl.ds(0, n), :], self.y_peer),
                self.copy(10, k, self.rows(k, self.b + self.mine, n), self.r4.at[slot, pl.ds(n, n), :], self.x_peer)]

    def c_mine_pair(self, k):
        return self.both(13, k, self.mine, self.n, self.z_peer)

    def c_mine_out(self, k):
        return self.both(15, k, self.mine, self.n, self.z_outer)

    def c_twin_out(self, k):
        return self.both(17, k, self.twin, self.n, self.z_outer)

    def c_mine_in(self, k):
        return self.both(11, k, self.mine, self.n, self.z_inner)

    def c_end_pair(self, k):
        return self.both(19, k, self.to_out, self.n, self.z_peer)

    def c_far_out(self, k):
        return self.both(21, k, self.far, self.n, self.z_outer)

    def c_wide(self, k):
        a, b = self.rows(k, self.a, self.q), self.rows(k, self.b, self.q)
        return [self.copy(23, k, a, a, self.x_peer), self.copy(24, k, b, b, self.y_peer)]

    def c_full(self, k):
        half = self.rows(k, self.own, self.half)
        return [self.copy(25, k, half, half, self.core_peer)]

    def go(self, make, k):
        for c in make(k):
            c.start()

    def go_lazy(self, make, k):
        @pl.when(k >= TURNS)
        def _():
            for c in make(k - TURNS):
                c.wait_send()

        self.go(make, k)

    def got(self, make, k):
        for c in make(k):
            c.wait_recv()

    def sent(self, make, k):
        for c in make(k):
            c.wait_send()

    def release(self, kind, peer):
        pl.semaphore_signal(self.free.at[kind], inc=1, device_id=peer, device_id_type=MESH)

    def add(self, k, at, src, src_row, count, scale=None):
        base = lax.rem(k, 2) * UNIT + at
        block = k // 2
        step = 16 if count % 16 == 0 else 8
        for i in range(0, count, step):
            rows = pl.ds(pl.multiple_of(base + i, 8), step)
            value = self.part[block, rows, :] + src[pl.ds(pl.multiple_of(src_row + i, 8), step), :]
            self.part[block, rows, :] = value if scale is None else value * scale

    def add_both(self, k, at, src, count):
        for e, base in enumerate((self.a, self.b)):
            self.add(k, base + at, src, e * self.q + at, count)

    def turn_done(self, k, r4):
        for c in self.c_turn(k):
            c.wait()
        self.add(k, self.a + self.mine, r4, 0, self.n, self.scale)
        self.add(k, self.b + self.mine, r4, self.n, self.n, self.scale)

    def stage(self, s, k):
        slot = lax.rem(k, SLOTS)
        r0, r1, r2, r3, r4 = (r.at[slot] for r in (self.r0, self.r1, self.r2, self.r3, self.r4))

        def on_inner(f):
            pl.when(self.inner)(f)

        def on_outer(f):
            pl.when(self.outer)(f)

        if s == 0:
            self.ready(k)
            self.go(self.c_core, k)
        elif s == 1:
            for c in self.c_core(k):
                c.wait()
            self.release(0, self.core_peer)
            self.add(k, self.own, r0, 0, self.half)
            self.go(self.c_side, k)
        elif s == 2:
            for c in self.c_side(k):
                c.wait()
            self.add(k, self.a, r1, 0, self.q)
            self.add(k, self.b, r1, self.q, self.q)

            @on_outer
            def _():
                self.go(self.c_in, k)
        elif s == 3:
            @on_inner
            def _():
                self.got(self.c_in, k)
                self.add_both(k, self.to_in, r2, 3 * self.n)
                self.go(self.c_pair, k)

            @on_outer
            def _():
                self.sent(self.c_in, k)
                self.release(1, self.z_inner)
        elif s == 4:
            @on_inner
            def _():
                for c in self.c_pair(k):
                    c.wait()
                self.release(2, self.z_peer)
                self.add_both(k, self.from_pair, r3, 2 * self.n)
                self.go(self.c_end, k)
                self.go(self.c_turn, k)
        elif s == 5:
            @on_inner
            def _():
                self.sent(self.c_end, k)
                self.release(3, self.z_outer)
                self.turn_done(k, r4)
                pl.semaphore_wait(self.free.at[1], 1)
                pl.semaphore_wait(self.free.at[2], 1)
                self.go_lazy(self.c_mine_pair, k)
                self.go_lazy(self.c_mine_out, k)

            @on_outer
            def _():
                self.got(self.c_end, k)
                self.add_both(k, self.mine, r2, self.n)
                self.go(self.c_turn, k)
        elif s == 6:
            @on_inner
            def _():
                self.got(self.c_mine_pair, k)
                self.go_lazy(self.c_twin_out, k)

            @on_outer
            def _():
                self.turn_done(k, r4)
                pl.semaphore_wait(self.free.at[3], 1)
                self.go_lazy(self.c_mine_in, k)
        elif s == 7:
            @on_inner
            def _():
                self.got(self.c_mine_in, k)
                self.go_lazy(self.c_end_pair, k)
        elif s == 8:
            @on_inner
            def _():
                self.got(self.c_end_pair, k)
                self.go_lazy(self.c_far_out, k)
                self.go_lazy(self.c_wide, k)
        elif s == 9:
            @on_outer
            def _():
                self.got(self.c_mine_out, k)
                self.got(self.c_twin_out, k)
                self.got(self.c_far_out, k)
                self.go_lazy(self.c_wide, k)
        elif s == 10:
            self.got(self.c_wide, k)
            pl.semaphore_wait(self.free.at[0], 1)
            self.go_lazy(self.c_full, k)
        elif s == 11:
            self.got(self.c_full, k)
            self.emit(k)

    def tick(self, t):
        for s in reversed(range(len(LAG))):
            k = t - LAG[s]

            @pl.when((k >= 0) & (k < self.total))
            def _():
                self.stage(s, k)

    def drain(self):
        def body(k, _):
            self.sent(self.c_wide, k)
            self.sent(self.c_full, k)

            @pl.when(self.inner)
            def _():
                for make in (self.c_mine_pair, self.c_mine_out, self.c_twin_out, self.c_end_pair, self.c_far_out):
                    self.sent(make, k)

            @pl.when(self.outer)
            def _():
                self.sent(self.c_mine_in, k)
            return 0

        lax.fori_loop(self.total - TURNS, self.total, body, 0)


def backward_kernel(groups, scale, *refs):
    (dw4, g_in, a3, h2, a1, h1, m_in, x0, w4, w3, w2, w1), refs = refs[:12], refs[12:]
    reduced, dm_out, refs = refs[0], refs[1], refs[2:]
    part, r0, r1, r2, r3, r4, d_act, w_down, w_up, g_buf, lhs, dh2, col = refs[:13]
    send, recv, free, load_sem, store_sem, side_sem, col_sem = refs[13:]
    total = 2 * sum(len(blocks_of(g)) for g in groups)

    def load(n, src, dst):
        return pltpu.make_async_copy(src, dst, side_sem.at[n])

    streams = ((a3, 0, 4), (h1, 4, 4), (a1, 8, 4), (x0, 12, 8))

    def fetch(n):
        for ref, first, count in streams:
            @pl.when((n >= first) & (n < first + count))
            def _():
                at = pl.ds(pl.multiple_of((n - first) * SIDE, SIDE), SIDE)
                slot = lax.rem(n, 2)
                pltpu.make_async_copy(ref.at[:, at], col.at[slot], col_sem.at[slot]).start()

    def fetched(n):
        slot = lax.rem(n, 2)
        pltpu.make_async_copy(a3.at[:, pl.ds(0, SIDE)], col.at[slot], col_sem.at[slot]).wait()
        return col.at[slot]

    load(0, g_in, g_buf).start()
    load(1, w4, w_down).start()
    fetch(0)
    load(2, h2, lhs).start()
    fetch(1)
    load(3, w3, w_up).start()
    for k in range(4):
        pltpu.make_async_copy(dw4.at[pl.ds(k * SIDE, SIDE), :], part.at[k], load_sem.at[k]).start()

    def ready(k):
        @pl.when((k < 8) & (lax.rem(k, 2) == 0))
        def _():
            pltpu.make_async_copy(dw4.at[pl.ds(0, SIDE), :], part.at[k // 2], load_sem.at[k // 2]).wait()

    def emit(k):
        rows = pl.ds(pl.multiple_of(lax.rem(k, 2) * UNIT, UNIT), UNIT)
        pltpu.make_async_copy(part.at[k // 2, rows, :], reduced.at[k // 2, rows, :], store_sem.at[k // 2, lax.rem(k, 2)]).start()

    def grad_block(k, left, right, right_cols):
        for piece in range(2):
            rows = pl.ds(piece * 1024, 1024)
            value = rows_contract(left[rows, :], right[rows, right_cols])
            if piece == 0:
                part[k] = value
            else:
                part[k] += value

    def slope_half(at, e, grad, act):
        def body(t, _):
            rows = pl.ds(pl.multiple_of(e * 1024 + t * 256, 256), 256)
            d_out = times_transposed(grad[rows, :], w_down[at, :]).astype(BF16)
            d_act[rows, at] = (d_out.astype(F32) * gelu_slope(act[rows, :])).astype(BF16)
            return 0

        lax.fori_loop(0, 4, body, 0)

    def back_half(e, add, dst):
        def body(t, _):
            rows = pl.ds(pl.multiple_of(e * 1024 + t * 512, 512), 512)
            dst[rows, :] = (times_transposed(d_act[rows, :], w_up[...]) + add[rows, :].astype(F32)).astype(BF16)
            return 0

        lax.fori_loop(0, 2, body, 0)

    def compute(t):
        @pl.when(t == 1)
        def _():
            load(0, g_in, g_buf).wait()
            load(1, w4, w_down).wait()
            load(2, h2, lhs).wait()

        @pl.when(t == 19)
        def _():
            load(4, w2, w_down).wait()
            load(5, m_in, lhs).wait()

        for first, n0, grad, k0 in ((1, 0, g_buf, 4), (19, 8, dh2, 12)):
            @pl.when((t >= first) & (t < first + 12))
            def _():
                j, r = (t - first) // 3, lax.rem(t - first, 3)
                at = pl.ds(pl.multiple_of(j * SIDE, SIDE), SIDE)

                @pl.when(r == 0)
                def _():
                    fetched(n0 + j)

                @pl.when(r < 2)
                def _():
                    slope_half(at, r, grad, col.at[lax.rem(n0 + j, 2)])

                @pl.when(r == 1)
                def _():
                    fetch(n0 + j + 2)

                @pl.when(r == 2)
                def _():
                    grad_block(k0 + j, lhs, d_act, at)

        @pl.when(t == 12)
        def _():
            load(4, w2, w_down).start()
            load(5, m_in, lhs).start()
            load(3, w3, w_up).wait()

        for first, add, dst in ((13, g_buf, dh2), (31, dh2, g_buf)):
            @pl.when((t >= first) & (t < first + 2))
            def _():
                back_half(t - first, add, dst)

        @pl.when(t == 14)
        def _():
            load(6, w1, w_up).start()

        @pl.when(t == 30)
        def _():
            load(6, w1, w_up).wait()

        @pl.when(t == 32)
        def _():
            load(7, g_buf, dm_out).start()

        @pl.when((t >= 15) & (t < 19))
        def _():
            left = fetched(t - 11)
            grad_block(t - 7, left, dh2, slice(None))
            fetch(t - 9)

        @pl.when((t >= 32) & (t < 48) & (lax.rem(t, 2) == 0))
        def _():
            j = (t - 32) // 2
            left = fetched(12 + j)
            grad_block(16 + j, left, g_buf, slice(None))
            fetch(14 + j)

    ex = Exchange(total, scale, part, r0, r1, r2, r3, r4, send, recv, free, ready, emit)
    ex.barrier()

    def step(i, _):
        compute(i)
        ex.tick(i)
        return 0

    lax.fori_loop(0, total + LAG[-1], step, 0)
    ex.drain()
    load(7, g_buf, dm_out).wait()

    def stored(k, _):
        rows = pl.ds(0, UNIT)
        pltpu.make_async_copy(part.at[0, rows, :], reduced.at[0, rows, :], store_sem.at[k // 2, lax.rem(k, 2)]).wait()
        return 0

    lax.fori_loop(0, total, stored, 0)


def backward(dw4, g, a3, h2, a1, h1, m, x0, w4, w3, w2, w1, groups, scale):
    total = sum(len(blocks_of(g)) for g in groups)
    any_spec = pl.BlockSpec(memory_space=pl.ANY)
    rows, wide = a3.shape
    return pl.pallas_call(
        functools.partial(backward_kernel, groups, scale),
        out_shape=[jax.ShapeDtypeStruct((total, SIDE, SIDE), F32), jax.ShapeDtypeStruct((rows, SIDE), BF16)],
        in_specs=[any_spec] * 12,
        out_specs=[any_spec] * 2,
        scratch_shapes=[
            pltpu.VMEM((total, SIDE, SIDE), F32),
            pltpu.VMEM((SLOTS, UNIT // 2, SIDE), F32),
            pltpu.VMEM((SLOTS, UNIT // 4, SIDE), F32),
            pltpu.VMEM((SLOTS, UNIT // 4, SIDE), F32),
            pltpu.VMEM((SLOTS, UNIT // 4, SIDE), F32),
            pltpu.VMEM((SLOTS, UNIT // 16, SIDE), F32),
            pltpu.VMEM((rows, wide), BF16),
            pltpu.VMEM((wide, SIDE), BF16),
            pltpu.VMEM((SIDE, wide), BF16),
            pltpu.VMEM((rows, SIDE), BF16),
            pltpu.VMEM((rows, SIDE), BF16),
            pltpu.VMEM((rows, SIDE), BF16),
            pltpu.VMEM((2, rows, SIDE), BF16),
            pltpu.SemaphoreType.DMA((26, TURNS)),
            pltpu.SemaphoreType.DMA((26, TURNS)),
            pltpu.SemaphoreType.REGULAR((4,)),
            pltpu.SemaphoreType.DMA((4,)),
            pltpu.SemaphoreType.DMA((total, 2)),
            pltpu.SemaphoreType.DMA((8,)),
            pltpu.SemaphoreType.DMA((2,)),
        ],
        compiler_params=pltpu.CompilerParams(
            collective_id=0, has_side_effects=True, vmem_limit_bytes=67 * 1000 * 1000),
        name="backward_and_mean",
    )(dw4, g, a3, h2, a1, h1, m, x0, w4, w3, w2, w1)


def finish_kernel(groups, reduced, dm_in, w0_in, dx, *refs):
    outs, (part, dm, w0, rows_out, load_sem, part_sem, in_sem, dx_sem) = refs[:5], refs[5:]
    loads = (pltpu.make_async_copy(dm_in, dm, in_sem.at[0]), pltpu.make_async_copy(w0_in, w0, in_sem.at[1]))
    for c in loads:
        c.start()
    stores = []
    fetches = [pltpu.make_async_copy(reduced.at[k], part.at[k], load_sem.at[k]) for k in range(part.shape[0])]
    for c in fetches:
        c.start()
    for ref, shape in zip(outs, groups):
        for r, c in blocks_of(shape):
            k = len(stores)
            stores.append(pltpu.make_async_copy(part.at[k], ref.at[pl.ds(r, SIDE), pl.ds(c, SIDE)], part_sem.at[k]))
    steps = w0.shape[0] // SIDE
    each = len(stores) // steps
    for c in loads:
        c.wait()

    def dx_copy(j):
        at = pl.ds(pl.multiple_of(j * SIDE, SIDE), SIDE)
        return pltpu.make_async_copy(rows_out.at[lax.rem(j, 2)], dx.at[:, at], dx_sem.at[lax.rem(j, 2)])

    for j in range(steps):
        for k in range(j * each, (j + 1) * each):
            fetches[k].wait()
            stores[k].start()
        if j >= 2:
            dx_copy(j - 2).wait()

        def piece(i, _):
            at = pl.ds(pl.multiple_of(i * 1024, 1024), 1024)
            rows_out[j % 2, at, :] = times_transposed(dm[at, :], w0[pl.ds(j * SIDE, SIDE), :]).astype(BF16)
            return 0

        lax.fori_loop(0, dm.shape[0] // 1024, piece, 0)
        dx_copy(j).start()
    for j in (steps - 2, steps - 1):
        dx_copy(j).wait()
    for c in stores:
        c.wait()


def finish(reduced, dm, w0, groups):
    any_spec = pl.BlockSpec(memory_space=pl.ANY)
    rows, wide = dm.shape[0], w0.shape[0]
    return pl.pallas_call(
        functools.partial(finish_kernel, groups),
        out_shape=[jax.ShapeDtypeStruct((rows, wide), BF16)] + [jax.ShapeDtypeStruct(g, F32) for g in groups],
        in_specs=[any_spec] * 3,
        out_specs=[any_spec] * 6,
        scratch_shapes=[
            pltpu.VMEM(reduced.shape, F32),
            pltpu.VMEM(dm.shape, BF16),
            pltpu.VMEM(w0.shape, BF16),
            pltpu.VMEM((2, rows, SIDE), BF16),
            pltpu.SemaphoreType.DMA((reduced.shape[0],)),
            pltpu.SemaphoreType.DMA((reduced.shape[0],)),
            pltpu.SemaphoreType.DMA((2,)),
            pltpu.SemaphoreType.DMA((2,)),
        ],
        compiler_params=pltpu.CompilerParams(vmem_limit_bytes=60 * 1000 * 1000),
        name="finish",
    )(reduced, dm, w0)


def solution(mesh):
    batch_axes = ("z", "y", "x")
    scale = 1.0 / mesh.size
    row_spec = P(batch_axes, None)
    full_spec = P(None, None)

    def device_step(x_in, g_out, w_in, w_up1, w_down1, w_up2, w_down2):
        x_mid = plain_product(x_in, w_in).astype(jnp.bfloat16)
        pre_one = plain_product(x_mid, w_up1).astype(jnp.bfloat16)
        act_one = gelu_value(pre_one).astype(jnp.bfloat16)
        hid_two = (plain_product(act_one, w_down1) + x_mid.astype(jnp.float32)).astype(jnp.bfloat16)
        pre_three = plain_product(hid_two, w_up2).astype(jnp.bfloat16)
        act_three = gelu_value(pre_three).astype(jnp.bfloat16)
        dw_down2 = rows_contract(act_three, g_out)
        groups = (dw_down2.shape, w_up2.shape, w_down1.shape, w_up1.shape, w_in.shape)
        reduced, d_mid = backward(
            dw_down2, g_out, pre_three, hid_two, pre_one, act_one, x_mid, x_in, w_down2, w_up2, w_down1, w_up1, groups, scale)
        dx_rows, dw_down2, dw_up2, dw_down1, dw_up1, dw_in = finish(reduced, d_mid, w_in, groups)
        return dx_rows, dw_in, dw_up1, dw_down1, dw_up2, dw_down2

    return jax.shard_map(
        device_step,
        mesh=mesh,
        in_specs=(row_spec, row_spec, full_spec, full_spec, full_spec, full_spec, full_spec),
        out_specs=(row_spec, full_spec, full_spec, full_spec, full_spec, full_spec),
        check_vma=False,
    )
```

time: 298 us -> 262 us (0.88)
  local copies, waits for them, and re-layouts: 27.7 us -> 6.65 us
  matrix products: 52.1 us -> 36.8 us
    pallas_call x0 -> x1, Pallas kernels: none -> 24.2 us  [finish(): pl.pallas_call(functools.partial(finish_kernel, groups), out_shape=[jax.S...]
    pallas_call x1, Pallas kernels: 217 us -> 193 us  [backward(): pl.pallas_call(functools.partial(backward_kernel, groups, scale), out_sha...]
    unnamed x29 -> x16, local copies, waits for them, and re-layouts: 27.7 us -> 6.65 us
    dot_general x1 -> x0, matrix products: 15 us -> none  [times_transposed(): lax.dot_general(first_op, second_op, (((1,), (1,)), ((), ())), preferred_...]
where the time goes in v1:
time: 262 us
  Pallas kernels  217 us (83%)
  matrix products  36.8 us (14%)
  local copies, waits for them, and re-layouts  6.65 us (3%)
    pallas_call x1, Pallas kernels, backward(): pl.pallas_call(functools.partial(backward_kernel, groups, scale), out_sha...  193 us
    dot_general x4, matrix products, plain_product(): lax.dot_general(first_op, second_op, (((1,), (0,)), ((), ())), preferred_...  30.6 us
    pallas_call x1, Pallas kernels, finish(): pl.pallas_call(functools.partial(finish_kernel, groups), out_shape=[jax.S...  24.2 us
    unnamed x16, local copies, waits for them, and re-layouts  6.65 us
    dot_general x1, matrix products, rows_contract(): lax.dot_general(first_op, second_op, (((0,), (0,)), ((), ())), preferred_...  6.18 us

profile of v1, /device:TPU:1, one launch (start us, length us, event | category | flops | bytes accessed | tf_op | source)
XLA Modules:
  0.0 261.7 jit_solution(15568815196378472119)
XLA Ops:
  0.6 0.0 copy-start.3
  0.6 13.7 %fusion.16.refs_6_ = bf16[2048,512]{1,0:T(8,128)(2,1)S(1)} fusion(bf16[2048,4096]{1,0:T(8,128)(2,1)} %refs_7_.1, bf16[4096,512]{1,0:T(8,128)(2,1)} %w0_in.1), kind=kOutput, calls=%fused_computation.22 | convolution fusion | flops 8589934592 | bytes 23068672 | tf_op jit(solution)/shard_map/dot_general | solution.py:33
  14.4 0.0 copy-done.3
  14.4 0.0 copy-start.6
  14.4 0.0 copy-start.4
  14.4 7.5 %fusion.1 = (bf16[2048,2048]{1,0:T(8,128)(2,1)S(1)}, bf16[2048,2048]{1,0:T(8,128)(2,1)}) fusion(bf16[2048,512]{1,0:T(8,128)(2,1)S(1)} %fusion.16.refs_6_, bf16[512,2048]{1,0:T(8,128)(2,1)S(1)} %copy-done.3), kind=kOutput, calls=%fused_computation.5 | convolution fusion | flops 4324327424 | bytes 20971520 | tf_op jit(solution)/shard_map/dot_general | solution.py:33
  21.9 0.0 copy-start
  21.9 0.0 copy-done.6
  21.9 3.2 %copy-done = bf16[2048,2048]{1,0:T(8,128)(2,1)} copy-done((bf16[2048,2048]{1,0:T(8,128)(2,1)}, bf16[2048,2048]{1,0:T(8,128)(2,1)S(1)}, u32[]{:S(2)}) %copy-start) | copy-done | bytes 8388632
  25.1 0.0 copy-done.4
  25.1 0.0 copy-start.5
  25.2 4.7 %fusion.12.refs_3_ = bf16[2048,512]{1,0:T(8,128)(2,1)S(1)} fusion(bf16[2048,512]{1,0:T(8,128)(2,1)S(1)} %fusion.16.refs_6_, bf16[2048,2048]{1,0:T(8,128)(2,1)S(1)} %get-tuple-element.22.refs_5_, bf16[2048,512]{1,0:T(8,128)(2,1)S(1)} %copy-done.4), kind=kOutput, calls=%fused_computation.18 | convolution fusion | flops 4298113024 | bytes 14680064 | tf_op jit(solution)/shard_map/dot_general | solution.py:33
  29.8 0.0 copy-done.5
  29.8 0.0 copy-start.7
  29.8 0.0 copy-start.2
  29.9 4.7 %convolution_convert_fusion.refs_2_ = bf16[2048,2048]{1,0:T(8,128)(2,1)S(1)} fusion(bf16[2048,512]{1,0:T(8,128)(2,1)S(1)} %fusion.12.refs_3_, bf16[512,2048]{1,0:T(8,128)(2,1)S(1)} %copy-done.5), kind=kOutput, calls=%fused_computation.13 | convolution fusion | flops 4299161600 | bytes 12582912 | tf_op jit(solution)/shard_map/dot_general | solution.py:33
  34.6 0.0 copy-done.7
  34.6 0.0 copy-start.1
  34.6 3.4 %copy-done.1 = bf16[2048,2048]{1,0:T(8,128)(2,1)} copy-done((bf16[2048,2048]{1,0:T(8,128)(2,1)}, bf16[2048,2048]{1,0:T(8,128)(2,1)S(1)}, u32[]{:S(2)}) %copy-start.1) | copy-done | bytes 8388632
  38.0 0.0 copy-done.2
  38.0 6.2 %fusion.8.refs_0_ = f32[2048,512]{1,0:T(8,128)} fusion(bf16[2048,512]{1,0:T(8,128)(2,1)S(1)} %copy-done.2, bf16[2048,2048]{1,0:T(8,128)(2,1)S(1)} %convolution_convert_fusion.refs_2_), kind=kOutput, calls=%fused_computation.12 | convolution fusion | flops 4320133120 | bytes 14680064 | tf_op jit(solution)/shard_map/dot_general | solution.py:37
  44.2 193.2 %backward_and_mean.1 = (f32[24,512,512]{2,1,0:T(8,128)}, bf16[2048,512]{1,0:T(8,128)(2,1)}) custom-call(f32[2048,512]{1,0:T(8,128)} %fusion.8.refs_0_, bf16[2048,512]{1,0:T(8,128)(2,1)} %refs_1_.1, bf16[2048,2048]{1,0:T(8,128)(2,1)} %copy-done.1, bf16[2048,512]{1,0:T(8,128)(2,1)} %copy-done.7, bf16[2048,2048]{1,0:T(8,128)(2,1)} %get-tuple-element.23.refs_4_, ...), custom_call_target="tpu_custom_call" | custom-call | tf_op jit(solution)/shard_map/backward_and_mean/pallas_call | solution.py:496
  237.4 24.2 %finish.1 = (bf16[2048,4096]{1,0:T(8,128)(2,1)}, f32[2048,512]{1,0:T(8,128)}, f32[512,2048]{1,0:T(8,128)}, f32[2048,512]{1,0:T(8,128)}, f32[512,2048]{1,0:T(8,128)}, /*index=5*/f32[4096,512]{1,0:T(8,128)}) custom-call(f32[24,512,512]{2,1,0:T(8,128)} %get-tuple-element.14.reduced, bf16[2048,512]{1,0:T(8,128)(2,1)} %get-tuple-element.15.dm_in, ...), custom_call_target="tpu_custom_call" | custom-call | tf_op jit(solution)/shard_map/finish/pallas_call | solution.py:574
Async XLA Ops:
  0.6 13.7 %copy-start.3 = (bf16[512,2048]{1,0:T(8,128)(2,1)S(1)}, bf16[512,2048]{1,0:T(8,128)(2,1)}, u32[]{:S(2)}) copy-start(bf16[512,2048]{1,0:T(8,128)(2,1)} %refs_11_.1) | copy-start | bytes 6291460
  14.4 7.6 %copy-start.6 = (bf16[2048,512]{1,0:T(8,128)(2,1)}, bf16[2048,512]{1,0:T(8,128)(2,1)S(1)}, u32[]{:S(2)}) copy-start(bf16[2048,512]{1,0:T(8,128)(2,1)S(1)} %fusion.16.refs_6_) | copy-start | bytes 6291460
  14.4 10.8 %copy-start.4 = (bf16[2048,512]{1,0:T(8,128)(2,1)S(1)}, bf16[2048,512]{1,0:T(8,128)(2,1)}, u32[]{:S(2)}) copy-start(bf16[2048,512]{1,0:T(8,128)(2,1)} %refs_10_.1) | copy-start | bytes 6291460
  21.9 3.2 %copy-start = (bf16[2048,2048]{1,0:T(8,128)(2,1)}, bf16[2048,2048]{1,0:T(8,128)(2,1)S(1)}, u32[]{:S(2)}) copy-start(bf16[2048,2048]{1,0:T(8,128)(2,1)S(1)} %get-tuple-element.22.refs_5_) | copy-start | bytes 25165828
  25.1 4.7 %copy-start.5 = (bf16[512,2048]{1,0:T(8,128)(2,1)S(1)}, bf16[512,2048]{1,0:T(8,128)(2,1)}, u32[]{:S(2)}) copy-start(bf16[512,2048]{1,0:T(8,128)(2,1)} %refs_9_.1) | copy-start | bytes 6291460
  29.8 4.8 %copy-start.7 = (bf16[2048,512]{1,0:T(8,128)(2,1)}, bf16[2048,512]{1,0:T(8,128)(2,1)S(1)}, u32[]{:S(2)}) copy-start(bf16[2048,512]{1,0:T(8,128)(2,1)S(1)} %fusion.12.refs_3_) | copy-start | bytes 6291460
  29.8 8.2 %copy-start.2 = (bf16[2048,512]{1,0:T(8,128)(2,1)S(1)}, bf16[2048,512]{1,0:T(8,128)(2,1)}, u32[]{:S(2)}) copy-start(bf16[2048,512]{1,0:T(8,128)(2,1)} %refs_1_.1) | copy-start | bytes 6291460
  34.6 3.4 %copy-start.1 = (bf16[2048,2048]{1,0:T(8,128)(2,1)}, bf16[2048,2048]{1,0:T(8,128)(2,1)S(1)}, u32[]{:S(2)}) copy-start(bf16[2048,2048]{1,0:T(8,128)(2,1)S(1)} %convolution_convert_fusion.refs_2_) | copy-start | bytes 25165828

commit v2 on v1

--- a/solution.py
+++ b/solution.py
@@ -16,7 +16,8 @@
 UNIT = SIDE // 2
 SLOTS = 8
 TURNS = 16
-LAG = (0, 2, 4, 6, 8, 10, 12, 14, 16, 18, 20, 22)
+LAG = (0, 1, 4, 6, 8, 11, 13, 14, 16, 19, 23, 25)
+TALL = 256
 
 
 def gelu_value(pre_act):
@@ -47,10 +48,10 @@
 
 
 class Exchange:
-    def __init__(self, total, scale, part, r0, r1, r2, r3, r4, send, recv, free, ready, emit):
+    def __init__(self, total, scale, part, r0, r1, r2, r3, r4, send, recv, free, emit):
         self.total, self.scale, self.part = total, scale, part
         self.r0, self.r1, self.r2, self.r3, self.r4 = r0, r1, r2, r3, r4
-        self.send, self.recv, self.free, self.ready, self.emit = send, recv, free, ready, emit
+        self.send, self.recv, self.free, self.emit = send, recv, free, emit
         z, y, x = lax.axis_index("z"), lax.axis_index("y"), lax.axis_index("x")
         core, chip = lax.rem(x, 2), x // 2
         self.core_peer = (z, y, chip * 2 + 1 - core)
@@ -214,7 +215,6 @@
             pl.when(self.outer)(f)
 
         if s == 0:
-            self.ready(k)
             self.go(self.c_core, k)
         elif s == 1:
             for c in self.c_core(k):
@@ -330,11 +330,45 @@
         lax.fori_loop(self.total - TURNS, self.total, body, 0)
 
 
+def forward_kernel(x, w0, w1, w2, w3, m, a1, h1, h2, a3, h3):
+    mid = plain_product(x[...], w0[...]).astype(BF16)
+    m[...] = mid
+    for c in range(0, w1.shape[1], SIDE):
+        at = pl.ds(c, SIDE)
+        pre = plain_product(mid, w1[:, at]).astype(BF16)
+        a1[:, at] = pre
+        h1[:, at] = gelu_value(pre).astype(BF16)
+    hid = (plain_product(h1[...], w2[...]) + mid.astype(F32)).astype(BF16)
+    h2[...] = hid
+    for c in range(0, w3.shape[1], SIDE):
+        at = pl.ds(c, SIDE)
+        pre = plain_product(hid, w3[:, at]).astype(BF16)
+        a3[:, at] = pre
+        h3[:, at] = gelu_value(pre).astype(BF16)
+
+
+def forward(x, w0, w1, w2, w3):
+    rows, deep = x.shape
+    side, wide = w1.shape
+    whole = lambda w: pl.BlockSpec(w.shape, lambda i: (0, 0), pipeline_mode=pl.Buffered(1))
+    tile = lambda width: pl.BlockSpec((TALL, width), lambda i: (i, 0))
+    widths = (side, wide, wide, side, wide, wide)
+    return pl.pallas_call(
+        forward_kernel,
+        grid=(rows // TALL,),
+        out_shape=[jax.ShapeDtypeStruct((rows, n), BF16) for n in widths],
+        in_specs=[tile(deep)] + [whole(w) for w in (w0, w1, w2, w3)],
+        out_specs=[tile(n) for n in widths],
+        compiler_params=pltpu.CompilerParams(vmem_limit_bytes=60 * 1000 * 1000),
+        name="forward",
+    )(x, w0, w1, w2, w3)
+
+
 def backward_kernel(groups, scale, *refs):
-    (dw4, g_in, a3, h2, a1, h1, m_in, x0, w4, w3, w2, w1), refs = refs[:12], refs[12:]
+    (h3, g_in, a3, h2, a1, h1, m_in, x0, w4, w3, w2, w1), refs = refs[:12], refs[12:]
     reduced, dm_out, refs = refs[0], refs[1], refs[2:]
-    part, r0, r1, r2, r3, r4, d_act, w_down, w_up, g_buf, lhs, dh2, col = refs[:13]
-    send, recv, free, load_sem, store_sem, side_sem, col_sem = refs[13:]
+    part, r0, r1, r2, r3, r4, d_act, w_down, w_up, g_buf, lhs, dh2, col, col3 = refs[:14]
+    send, recv, free, store_sem, side_sem, col_sem, col3_sem = refs[14:]
     total = 2 * sum(len(blocks_of(g)) for g in groups)
 
     def load(n, src, dst):
@@ -355,19 +389,18 @@
         pltpu.make_async_copy(a3.at[:, pl.ds(0, SIDE)], col.at[slot], col_sem.at[slot]).wait()
         return col.at[slot]
 
+    def h3_copy(j):
+        at = pl.ds(pl.multiple_of(j * SIDE, SIDE), SIDE)
+        return pltpu.make_async_copy(h3.at[:, at], col3.at[lax.rem(j, 2)], col3_sem.at[lax.rem(j, 2)])
+
     load(0, g_in, g_buf).start()
+    h3_copy(0).start()
     load(1, w4, w_down).start()
     fetch(0)
+    h3_copy(1).start()
     load(2, h2, lhs).start()
     fetch(1)
     load(3, w3, w_up).start()
-    for k in range(4):
-        pltpu.make_async_copy(dw4.at[pl.ds(k * SIDE, SIDE), :], part.at[k], load_sem.at[k]).start()
-
-    def ready(k):
-        @pl.when((k < 8) & (lax.rem(k, 2) == 0))
-        def _():
-            pltpu.make_async_copy(dw4.at[pl.ds(0, SIDE), :], part.at[k // 2], load_sem.at[k // 2]).wait()
 
     def emit(k):
         rows = pl.ds(pl.multiple_of(lax.rem(k, 2) * UNIT, UNIT), UNIT)
@@ -400,9 +433,22 @@
         lax.fori_loop(0, 2, body, 0)
 
     def compute(t):
+        @pl.when(t == 0)
+        def _():
+            load(0, g_in, g_buf).wait()
+
+        @pl.when((t < 8) & (lax.rem(t, 2) == 0))
+        def _():
+            j = t // 2
+            h3_copy(j).wait()
+            grad_block(j, col3.at[lax.rem(j, 2)], g_buf, slice(None))
+
+            @pl.when(j < 2)
+            def _():
+                h3_copy(j + 2).start()
+
         @pl.when(t == 1)
         def _():
-            load(0, g_in, g_buf).wait()
             load(1, w4, w_down).wait()
             load(2, h2, lhs).wait()
 
@@ -469,7 +515,7 @@
             grad_block(16 + j, left, g_buf, slice(None))
             fetch(14 + j)
 
-    ex = Exchange(total, scale, part, r0, r1, r2, r3, r4, send, recv, free, ready, emit)
+    ex = Exchange(total, scale, part, r0, r1, r2, r3, r4, send, recv, free, emit)
     ex.barrier()
 
     def step(i, _):
@@ -489,7 +535,7 @@
     lax.fori_loop(0, total, stored, 0)
 
 
-def backward(dw4, g, a3, h2, a1, h1, m, x0, w4, w3, w2, w1, groups, scale):
+def backward(h3, g, a3, h2, a1, h1, m, x0, w4, w3, w2, w1, groups, scale):
     total = sum(len(blocks_of(g)) for g in groups)
     any_spec = pl.BlockSpec(memory_space=pl.ANY)
     rows, wide = a3.shape
@@ -512,18 +558,19 @@
             pltpu.VMEM((rows, SIDE), BF16),
             pltpu.VMEM((rows, SIDE), BF16),
             pltpu.VMEM((2, rows, SIDE), BF16),
+            pltpu.VMEM((2, rows, SIDE), BF16),
             pltpu.SemaphoreType.DMA((26, TURNS)),
             pltpu.SemaphoreType.DMA((26, TURNS)),
             pltpu.SemaphoreType.REGULAR((4,)),
-            pltpu.SemaphoreType.DMA((4,)),
             pltpu.SemaphoreType.DMA((total, 2)),
             pltpu.SemaphoreType.DMA((8,)),
+            pltpu.SemaphoreType.DMA((2,)),
             pltpu.SemaphoreType.DMA((2,)),
         ],
         compiler_params=pltpu.CompilerParams(
             collective_id=0, has_side_effects=True, vmem_limit_bytes=67 * 1000 * 1000),
         name="backward_and_mean",
-    )(dw4, g, a3, h2, a1, h1, m, x0, w4, w3, w2, w1)
+    )(h3, g, a3, h2, a1, h1, m, x0, w4, w3, w2, w1)
 
 
 def finish_kernel(groups, reduced, dm_in, w0_in, dx, *refs):
@@ -598,16 +645,10 @@
     full_spec = P(None, None)
 
     def device_step(x_in, g_out, w_in, w_up1, w_down1, w_up2, w_down2):
-        x_mid = plain_product(x_in, w_in).astype(jnp.bfloat16)
-        pre_one = plain_product(x_mid, w_up1).astype(jnp.bfloat16)
-        act_one = gelu_value(pre_one).astype(jnp.bfloat16)
-        hid_two = (plain_product(act_one, w_down1) + x_mid.astype(jnp.float32)).astype(jnp.bfloat16)
-        pre_three = plain_product(hid_two, w_up2).astype(jnp.bfloat16)
-        act_three = gelu_value(pre_three).astype(jnp.bfloat16)
-        dw_down2 = rows_contract(act_three, g_out)
-        groups = (dw_down2.shape, w_up2.shape, w_down1.shape, w_up1.shape, w_in.shape)
+        x_mid, pre_one, act_one, hid_two, pre_three, act_three = forward(x_in, w_in, w_up1, w_down1, w_up2)
+        groups = (w_down2.shape, w_up2.shape, w_down1.shape, w_up1.shape, w_in.shape)
         reduced, d_mid = backward(
-            dw_down2, g_out, pre_three, hid_two, pre_one, act_one, x_mid, x_in, w_down2, w_up2, w_down1, w_up1, groups, scale)
+            act_three, g_out, pre_three, hid_two, pre_one, act_one, x_mid, x_in, w_down2, w_up2, w_down1, w_up1, groups, scale)
         dx_rows, dw_down2, dw_up2, dw_down1, dw_up1, dw_in = finish(reduced, d_mid, w_in, groups)
         return dx_rows, dw_in, dw_up1, dw_down1, dw_up2, dw_down2
 

time: 262 us -> 251 us (0.958)
  matrix products: 36.8 us -> 0 us
  Pallas kernels: 217 us -> 250 us
  local copies, waits for them, and re-layouts: 6.65 us -> 0 us
    dot_general x5 -> x0, matrix products: 36.8 us -> none  [the longest x4 30.6 us: plain_product(): lax.dot_general(first_op, second_op, (((1,), (0,)), ((), ())), preferred_...]
    pallas_call x0 -> x1, Pallas kernels: none -> 33.2 us  [forward(): pl.pallas_call(forward_kernel, grid=(rows // TALL,), out_shape=[jax.Shape...]
    unnamed x16 -> x0, local copies, waits for them, and re-layouts: 6.65 us -> none
where the time goes in v2:
time: 251 us
  Pallas kernels  250 us (100%)
    pallas_call x1, Pallas kernels, backward(): pl.pallas_call(functools.partial(backward_kernel, groups, scale), out_sha...  193 us
    pallas_call x1, Pallas kernels, forward(): pl.pallas_call(forward_kernel, grid=(rows // TALL,), out_shape=[jax.Shape...  33.2 us
    pallas_call x1, Pallas kernels, finish(): pl.pallas_call(functools.partial(finish_kernel, groups), out_shape=[jax.S...  24.2 us

profile of v2, /device:TPU:1, one launch (start us, length us, event | category | flops | bytes accessed | tf_op | source)
XLA Modules:
  0.0 251.3 jit_solution(15727668760495509450)
XLA Ops:
  0.6 33.2 %forward.1 = (bf16[2048,512]{1,0:T(8,128)(2,1)}, bf16[2048,2048]{1,0:T(8,128)(2,1)}, bf16[2048,2048]{1,0:T(8,128)(2,1)}, bf16[2048,512]{1,0:T(8,128)(2,1)}, bf16...) custom-call(bf16[2048,4096]{1,0:T(8,128)(2,1)} %refs_7_.1, bf16[4096,512]{1,0:T(8,128)(2,1)} %w0_in.1, ...), custom_call_target="tpu_custom_call" | custom-call | tf_op jit(solution)/shard_map/forward/pallas_call | solution.py:356
  33.9 193.1 %backward_and_mean.1 = (f32[24,512,512]{2,1,0:T(8,128)}, bf16[2048,512]{1,0:T(8,128)(2,1)}) custom-call(bf16[2048,2048]{1,0:T(8,128)(2,1)} %get-tuple-element.20.refs_0_, bf16[2048,512]{1,0:T(8,128)(2,1)} %refs_1_.1, bf16[2048,2048]{1,0:T(8,128)(2,1)} %get-tuple-element.21.refs_2_, bf16[2048,512]{1,0:T(8,128)(2,1)} %get-tuple-element.22.refs_3_, ...), custom_call_target="tpu_custom_call" | custom-call | tf_op jit(solution)/shard_map/backward_and_mean/pallas_call | solution.py:542
  227.0 24.2 %finish.1 = (bf16[2048,4096]{1,0:T(8,128)(2,1)}, f32[2048,512]{1,0:T(8,128)}, f32[512,2048]{1,0:T(8,128)}, f32[2048,512]{1,0:T(8,128)}, f32[512,2048]{1,0:T(8,128)}, /*index=5*/f32[4096,512]{1,0:T(8,128)}) custom-call(f32[24,512,512]{2,1,0:T(8,128)} %get-tuple-element.26.reduced, bf16[2048,512]{1,0:T(8,128)(2,1)} %get-tuple-element.27.dm_in, ...), custom_call_target="tpu_custom_call" | custom-call | tf_op jit(solution)/shard_map/finish/pallas_call | solution.py:621

commit v3 on v2

--- a/solution.py
+++ b/solution.py
@@ -422,7 +422,7 @@
             d_act[rows, at] = (d_out.astype(F32) * gelu_slope(act[rows, :])).astype(BF16)
             return 0
 
-        lax.fori_loop(0, 4, body, 0)
+        lax.fori_loop(0, 4, body, 0, unroll=True)
 
     def back_half(e, add, dst):
         def body(t, _):

time: 251 us -> 249 us (level)
    pallas_call x1, Pallas kernels: 193 us -> 190 us  [backward(): pl.pallas_call(functools.partial(backward_kernel, groups, scale), out_sha...]
where the time goes in v3:
time: 249 us; the launch traced here: 248 us
  Pallas kernels  248 us (100%)
    pallas_call x1, Pallas kernels, backward(): pl.pallas_call(functools.partial(backward_kernel, groups, scale), out_sha...  190 us
    pallas_call x1, Pallas kernels, forward(): pl.pallas_call(forward_kernel, grid=(rows // TALL,), out_shape=[jax.Shape...  33.2 us
    pallas_call x1, Pallas kernels, finish(): pl.pallas_call(functools.partial(finish_kernel, groups), out_shape=[jax.S...  24.1 us

profile of v3, /device:TPU:1, one launch (start us, length us, event | category | flops | bytes accessed | tf_op | source)
XLA Modules:
  0.0 248.4 jit_solution(17102760187892681265)
XLA Ops:
  0.6 33.2 %forward.1 = (bf16[2048,512]{1,0:T(8,128)(2,1)}, bf16[2048,2048]{1,0:T(8,128)(2,1)}, bf16[2048,2048]{1,0:T(8,128)(2,1)}, bf16[2048,512]{1,0:T(8,128)(2,1)}, bf16...) custom-call(bf16[2048,4096]{1,0:T(8,128)(2,1)} %refs_7_.1, bf16[4096,512]{1,0:T(8,128)(2,1)} %w0_in.1, ...), custom_call_target="tpu_custom_call" | custom-call | tf_op jit(solution)/shard_map/forward/pallas_call | solution.py:356
  33.9 190.2 %backward_and_mean.1 = (f32[24,512,512]{2,1,0:T(8,128)}, bf16[2048,512]{1,0:T(8,128)(2,1)}) custom-call(bf16[2048,2048]{1,0:T(8,128)(2,1)} %get-tuple-element.20.refs_0_, bf16[2048,512]{1,0:T(8,128)(2,1)} %refs_1_.1, bf16[2048,2048]{1,0:T(8,128)(2,1)} %get-tuple-element.21.refs_2_, bf16[2048,512]{1,0:T(8,128)(2,1)} %get-tuple-element.22.refs_3_, ...), custom_call_target="tpu_custom_call" | custom-call | tf_op jit(solution)/shard_map/backward_and_mean/pallas_call | solution.py:542
  224.0 24.1 %finish.1 = (bf16[2048,4096]{1,0:T(8,128)(2,1)}, f32[2048,512]{1,0:T(8,128)}, f32[512,2048]{1,0:T(8,128)}, f32[2048,512]{1,0:T(8,128)}, f32[512,2048]{1,0:T(8,128)}, /*index=5*/f32[4096,512]{1,0:T(8,128)}) custom-call(f32[24,512,512]{2,1,0:T(8,128)} %get-tuple-element.26.reduced, bf16[2048,512]{1,0:T(8,128)(2,1)} %get-tuple-element.27.dm_in, ...), custom_call_target="tpu_custom_call" | custom-call | tf_op jit(solution)/shard_map/finish/pallas_call | solution.py:621
